TPU v7x, 32 devices: a whole 2x2x4 slice. The times are simulated.
32 devices in a mesh: pb: 4 (over z), ka: 8 (over y, x, core).
Axes of the slice: x: 2, y: 2, z: 4, core: 2. Of those that a mesh axis runs over, the one named last changes fastest.
Arguments:
- queries: float32 [1, 4096, 128], P(None, ('pb', 'ka')), may hold values from -6 to 6
- keys: float32 [1, 4096, 128], P(None, ('ka', 'pb')), may hold values from -6 to 6
- values: float32 [1, 4096, 128], P(None, ('ka', 'pb')), may hold values from -6 to 6
- tangent_q: float32 [1, 4096, 128], P(None, ('pb', 'ka')), may hold values from -6 to 6
- tangent_k: float32 [1, 4096, 128], P(None, ('ka', 'pb')), may hold values from -6 to 6
- tangent_v: float32 [1, 4096, 128], P(None, ('ka', 'pb')), may hold values from -6 to 6
Outputs:
- attended: float32 [1, 4096, 128], P(None, ('pb', 'ka'))
- attended_tangent: float32 [1, 4096, 128], P(None, ('pb', 'ka'))
All inputs are finite; a program needn't handle non-finite values.
Results may differ from a plain program's by a relative error of at most 0.0003.
Values sent between devices are 32-bit elements; how exact they have to be, the bound alone decides.
No kernel may reach another device: no remote copies, remote signals or barrier semaphores. Data moves between devices by JAX's collectives and lax.ppermute only.
A program may use at most 128 MiB of HBM per device.

v0:
```python
import jax
import jax.numpy as jnp
from jax import lax
from jax.sharding import PartitionSpec as P


def combined_all(value, axis, join):
    pieces = jax.tree.map(lambda part: lax.all_gather(part, axis), value)
    head = jax.tree.map(lambda part: part[0], pieces)
    tail = jax.tree.map(lambda part: part[1:], pieces)
    so_far, _ = lax.scan(lambda so_far, share: (join(so_far, share), None), head, tail)
    return so_far


def join_partials(first, second):
    peak = jnp.maximum(first[0], second[0])
    left = jnp.exp(first[0] - peak)
    right = jnp.exp(second[0] - peak)
    total = first[1] * left + second[1] * right
    numer = first[2] * left[..., None] + second[2] * right[..., None]
    tnumer = first[3] * left[..., None] + second[3] * right[..., None]
    drift = first[4] * left + second[4] * right
    return (peak, total, numer, tnumer, drift)


def body(queries, keys, values, tangent_q, tangent_k, tangent_v):
    highest = lax.Precision.HIGHEST
    head_count, _, width = queries.shape
    factor = width ** (-0.5)
    all_q, all_dq = (
        lax.all_gather(queries, "ka", axis=1, tiled=True),
        lax.all_gather(tangent_q, "ka", axis=1, tiled=True),
    )
    span = all_q.shape[1]
    block = min(512, span)
    blocks = span // block
    split_q = all_q.reshape(head_count, blocks, block, width)
    split_dq = all_dq.reshape(head_count, blocks, block, width)
    start_state = (
        jnp.full((head_count, span), -1e30, jnp.float32),
        jnp.zeros((head_count, span), jnp.float32),
        jnp.zeros((head_count, span, width), jnp.float32),
        jnp.zeros((head_count, span, width), jnp.float32),
        jnp.zeros((head_count, span), jnp.float32),
    )
    piece_k = lax.all_gather(keys, "pb", axis=1, tiled=True)
    piece_dk = lax.all_gather(tangent_k, "pb", axis=1, tiled=True)
    piece_v = lax.all_gather(values, "pb", axis=1, tiled=True)
    piece_dv = lax.all_gather(tangent_v, "pb", axis=1, tiled=True)
    shaped = (
        start_state[0].reshape(head_count, blocks, block),
        start_state[1].reshape(head_count, blocks, block),
        start_state[2].reshape(head_count, blocks, block, width),
        start_state[3].reshape(head_count, blocks, block, width),
        start_state[4].reshape(head_count, blocks, block),
    )

    def one_head(items):
        (
            head_q,
            head_dq,
            head_k,
            head_dk,
            head_v,
            head_dv,
            peak_h,
            total_h,
            numer_h,
            tnumer_h,
            drift_h,
        ) = items

        def one_block(parts):
            query_blk, dquery_blk, old_peak, old_total, old_numer, old_tnumer, old_drift = parts
            scores = jnp.dot(query_blk, head_k.T, precision=highest) * factor
            tangent = (
                jnp.dot(dquery_blk, head_k.T, precision=highest)
                + jnp.dot(query_blk, head_dk.T, precision=highest)
            ) * factor
            new_peak = jnp.maximum(old_peak, jnp.max(scores, axis=1))
            rescale = jnp.exp(old_peak - new_peak)
            weights = jnp.exp(scores - new_peak[:, None])
            product = weights * tangent
            new_total = old_total * rescale + jnp.sum(weights, axis=1)
            new_numer = old_numer * rescale[:, None] + jnp.dot(weights, head_v, precision=highest)
            new_tnumer = (
                old_tnumer * rescale[:, None]
                + jnp.dot(weights, head_dv, precision=highest)
                + jnp.dot(product, head_v, precision=highest)
            )
            new_drift = old_drift * rescale + jnp.sum(product, axis=1)
            return (new_peak, new_total, new_numer, new_tnumer, new_drift)

        return lax.map(one_block, (head_q, head_dq, peak_h, total_h, numer_h, tnumer_h, drift_h))

    result = lax.map(one_head, (split_q, split_dq, piece_k, piece_dk, piece_v, piece_dv) + shaped)
    peak = result[0].reshape(head_count, span)
    total = result[1].reshape(head_count, span)
    numer = result[2].reshape(head_count, span, width)
    tnumer = result[3].reshape(head_count, span, width)
    drift = result[4].reshape(head_count, span)
    merged = combined_all((peak, total, numer, tnumer, drift), "ka", join_partials)
    owned = span // lax.axis_size("ka")
    offset = lax.axis_index("ka") * owned
    total = lax.dynamic_slice_in_dim(merged[1], offset, owned, 1)
    numer = lax.dynamic_slice_in_dim(merged[2], offset, owned, 1)
    tnumer = lax.dynamic_slice_in_dim(merged[3], offset, owned, 1)
    drift = lax.dynamic_slice_in_dim(merged[4], offset, owned, 1)
    attended = numer / total[..., None]
    attended_tangent = tnumer / total[..., None] - attended * (drift / total)[..., None]
    return (attended, attended_tangent)


def solution(mesh):
    return jax.shard_map(
        body,
        mesh=mesh,
        in_specs=(
            P(None, ("pb", "ka"), None),
            P(None, ("ka", "pb"), None),
            P(None, ("ka", "pb"), None),
            P(None, ("pb", "ka"), None),
            P(None, ("ka", "pb"), None),
            P(None, ("ka", "pb"), None),
        ),
        out_specs=(P(None, ("pb", "ka"), None), P(None, ("pb", "ka"), None)),
        check_vma=False,
    )
```

profile of v0, /device:TPU:0, one launch (start us, length us, event | category | flops | bytes accessed | tf_op | source)
XLA Modules:
  0.0 214.0 jit_solution(3527905628978141757)
XLA Ops:
  7.3 15.9 %all_gather.34 = f32[1,512,128]{2,1,0:T(8,128)S(1)} all-gather(f32[1,128,128]{2,1,0:T(8,128)} %param.11), channel_id=1, replica_groups=mesh['pb'=4,'ka'=8] {'pb'}, dimensions={1}, use_global_device_ids=true | all-gather | bytes 327680 | tf_op jit(solution)/shard_map/all_gather | solution.py:46
  23.1 14.9 %all_gather.35 = f32[1,512,128]{2,1,0:T(8,128)S(1)} all-gather(f32[1,128,128]{2,1,0:T(8,128)} %param.12), channel_id=1, replica_groups=mesh['pb'=4,'ka'=8] {'pb'}, dimensions={1}, use_global_device_ids=true | all-gather | bytes 327680 | tf_op jit(solution)/shard_map/all_gather | solution.py:48
  38.0 14.0 %all_gather.38 = f32[1,512,128]{2,1,0:T(8,128)S(1)} all-gather(f32[1,128,128]{2,1,0:T(8,128)} %param.14), channel_id=1, replica_groups=mesh['pb'=4,'ka'=8] {'pb'}, dimensions={1}, use_global_device_ids=true | all-gather | bytes 327680 | tf_op jit(solution)/shard_map/all_gather | solution.py:47
  52.1 16.6 %all_gather.36 = f32[1,512,128]{2,1,0:T(8,128)} all-gather(f32[1,128,128]{2,1,0:T(8,128)} %param.15), channel_id=1, replica_groups=mesh['pb'=4,'ka'=8] {'pb'}, dimensions={1}, use_global_device_ids=true | all-gather | bytes 327680 | tf_op jit(solution)/shard_map/all_gather | solution.py:49
  68.6 10.1 %all_gather.33 = f32[1,1024,128]{2,1,0:T(8,128)S(1)} all-gather(f32[1,128,128]{2,1,0:T(8,128)} %param.10), channel_id=1, replica_groups=mesh['pb'=4,'ka'=8] {'ka'}, dimensions={1}, use_global_device_ids=true | all-gather | bytes 589824 | tf_op jit(solution)/shard_map/all_gather | solution.py:31
  78.8 10.8 %all_gather.37 = f32[1,1024,128]{2,1,0:T(8,128)} all-gather(f32[1,128,128]{2,1,0:T(8,128)} %param.13), channel_id=1, replica_groups=mesh['pb'=4,'ka'=8] {'ka'}, dimensions={1}, use_global_device_ids=true | all-gather | bytes 589824 | tf_op jit(solution)/shard_map/all_gather | solution.py:32
  89.5 24.6 %while.53 = (s32[]{:T(128)}, f32[2,512]{1,0:T(2,128)S(1)}, f32[2,512]{1,0:T(2,128)S(1)}, f32[2,512,128]{2,1,0:T(8,128)}, f32[2,512,128]{2,1,0:T(8,128)}, /*index...) while((s32[]{:T(128)}, f32[2,512]{1,0:T(2,128)S(1)}, ...), condition=%wide.region_4.5_spmd, body=%wide.region_0.4_spmd.sunk | while | flops 2419001344 | bytes 12892333 | solution.py:94
  89.5 1.9 fusion.66
  92.7 1.2 fusion.67
  94.0 2.8 %convolution_add_fusion.5 = f32[512,128]{1,0:T(8,128)S(1)} fusion(f32[512,128]{1,0:T(8,128)} %get-tuple-element.549, f32[512,512]{0,1:T(8,128)S(1)} %get-tuple-element.489, f32[512]{0:T(512)S(1)} %get-tuple-element.488, f32[512]{0:T(512)S(1)} %get-tuple-element.492), kind=kOutput, calls=%fused_computation.7.clone.1 | convolution fusion | flops 402980864 | bytes 1576960 | tf_op jit(solution)/shard_map/while/body/eval_jaxpr/while/body/eval_jaxpr/dot_general | solution.py:88
  96.8 2.5 %fusion.71 = f32[2,512,128]{2,1,0:T(8,128)} fusion(f32[2,512,128]{2,1,0:T(8,128)} %get-tuple-element.530, s32[]{:T(128)S(6)} %copy.19, f32[512,128]{1,0:T(8,128)S(1)} %convolution_add_fusion.5, f32[512,512]{0,1:T(8,128)S(1)} %get-tuple-element.493, f32[512,128]{1,0:T(8,128)S(1)} %get-tuple-element.548), kind=kOutput, calls=%fused_computation.6.clone.1 | convolution fusion | flops 402718720 | bytes 1835012 | tf_op jit(solution)/shard_map/while/body/eval_jaxpr/while/body/eval_jaxpr/dot_general | solution.py:89
  99.3 2.5 %fusion.70 = f32[2,512,128]{2,1,0:T(8,128)} fusion(f32[2,512,128]{2,1,0:T(8,128)} %get-tuple-element.529, s32[]{:T(128)S(6)} %copy.19, f32[512,128]{1,0:T(8,128)S(1)} %get-tuple-element.548, f32[512,512]{0,1:T(8,128)S(1)} %get-tuple-element.489, f32[512]{0:T(512)S(1)} %get-tuple-element.488, f32[512]{0:T(512)S(1)} %get-tuple-element.492), kind=kOutput, calls=%fused_computation.10.clone.1 | convolution fusion | flops 402980864 | bytes 1576964 | tf_op jit(solution)/shard_map/while/body/eval_jaxpr/while/body/eval_jaxpr/dot_general | solution.py:85
  101.9 1.9 fusion.66
  105.1 1.2 fusion.67
  106.4 2.8 %convolution_add_fusion.5 = f32[512,128]{1,0:T(8,128)S(1)} fusion(f32[512,128]{1,0:T(8,128)} %get-tuple-element.549, f32[512,512]{0,1:T(8,128)S(1)} %get-tuple-element.489, f32[512]{0:T(512)S(1)} %get-tuple-element.488, f32[512]{0:T(512)S(1)} %get-tuple-element.492), kind=kOutput, calls=%fused_computation.7.clone.1 | convolution fusion | flops 402980864 | bytes 1576960 | tf_op jit(solution)/shard_map/while/body/eval_jaxpr/while/body/eval_jaxpr/dot_general | solution.py:88
  109.1 2.5 %fusion.71 = f32[2,512,128]{2,1,0:T(8,128)} fusion(f32[2,512,128]{2,1,0:T(8,128)} %get-tuple-element.530, s32[]{:T(128)S(6)} %copy.19, f32[512,128]{1,0:T(8,128)S(1)} %convolution_add_fusion.5, f32[512,512]{0,1:T(8,128)S(1)} %get-tuple-element.493, f32[512,128]{1,0:T(8,128)S(1)} %get-tuple-element.548), kind=kOutput, calls=%fused_computation.6.clone.1 | convolution fusion | flops 402718720 | bytes 1835012 | tf_op jit(solution)/shard_map/while/body/eval_jaxpr/while/body/eval_jaxpr/dot_general | solution.py:89
  111.7 2.5 %fusion.70 = f32[2,512,128]{2,1,0:T(8,128)} fusion(f32[2,512,128]{2,1,0:T(8,128)} %get-tuple-element.529, s32[]{:T(128)S(6)} %copy.19, f32[512,128]{1,0:T(8,128)S(1)} %get-tuple-element.548, f32[512,512]{0,1:T(8,128)S(1)} %get-tuple-element.489, f32[512]{0:T(512)S(1)} %get-tuple-element.488, f32[512]{0:T(512)S(1)} %get-tuple-element.492), kind=kOutput, calls=%fused_computation.10.clone.1 | convolution fusion | flops 402980864 | bytes 1576964 | tf_op jit(solution)/shard_map/while/body/eval_jaxpr/while/body/eval_jaxpr/dot_general | solution.py:85
  115.0 8.8 %all_gather.40 = f32[8,1,1024]{2,1,0:T(1,128)S(1)} all-gather(f32[1,1,1024]{2,1,0:T(1,128)S(1)} %all_gather_reshape.16), channel_id=1, replica_groups=mesh['pb'=4,'ka'=8] {'ka'}, dimensions={0}, use_global_device_ids=true | all-gather | bytes 36864 | tf_op jit(solution)/shard_map/all_gather | solution.py:8
  123.8 8.6 %all_gather.39 = f32[8,1,1024]{2,1,0:T(1,128)S(1)} all-gather(f32[1,1,1024]{2,1,0:T(1,128)S(1)} %all_gather_reshape.15), channel_id=1, replica_groups=mesh['pb'=4,'ka'=8] {'ka'}, dimensions={0}, use_global_device_ids=true | all-gather | bytes 36864 | tf_op jit(solution)/shard_map/all_gather | solution.py:8
  132.4 9.0 %all_gather.43 = f32[8,1,1024]{2,1,0:T(1,128)S(1)} all-gather(f32[1,1,1024]{2,1,0:T(1,128)S(1)} %all_gather_reshape.19), channel_id=1, replica_groups=mesh['pb'=4,'ka'=8] {'ka'}, dimensions={0}, use_global_device_ids=true | all-gather | bytes 36864 | tf_op jit(solution)/shard_map/all_gather | solution.py:8
  141.4 8.8 %all-gather.5.cloned.1.call-done = f32[8,1,1024,128]{3,2,1,0:T(8,128)} async-done(((f32[1,1,1024,128]{3,2,1,0:T(8,128)}), f32[8,1,1024,128]{3,2,1,0:T(8,128)}) %all-gather.5.cloned.1.call-update) | async-done | bytes 4194320 | tf_op jit(solution)/shard_map/all_gather | solution.py:8
  150.2 4.1 %slice.48 = f32[7,1,1024,128]{3,2,1,0:T(8,128)} slice(f32[8,1,1024,128]{3,2,1,0:T(8,128)} %all-gather.5.cloned.1.call-done), slice={[1:8], [0:1], [0:1024], [0:128]} | slice | bytes 7340032 | tf_op jit(solution)/shard_map/slice | solution.py:10
  155.4 33.3 %all-gather.3.cloned.1.call-done = f32[8,1,1024,128]{3,2,1,0:T(8,128)} async-done(((f32[1,1,1024,128]{3,2,1,0:T(8,128)}), f32[8,1,1024,128]{3,2,1,0:T(8,128)}) %all-gather.3.cloned.1.call-update) | async-done | bytes 4194320 | tf_op jit(solution)/shard_map/all_gather | solution.py:8
  189.8 4.1 %slice.47 = f32[7,1,1024,128]{3,2,1,0:T(8,128)} slice(f32[8,1,1024,128]{3,2,1,0:T(8,128)} %all-gather.3.cloned.1.call-done), slice={[1:8], [0:1], [0:1024], [0:128]} | slice | bytes 7340032 | tf_op jit(solution)/shard_map/slice | solution.py:10
  193.8 12.5 %while.54 = (s32[]{:T(128)}, f32[1,1024]{1,0:T(1,128)S(1)}, f32[1,1024]{1,0:T(1,128)S(1)}, f32[1,1024,128]{2,1,0:T(8,128)S(1)}, f32[1,1024,128]{2,1,0:T(8,128)S(...) while((s32[]{:T(128)}, f32[1,1024]{1,0:T(1,128)S(1)}, ...), condition=%wide.region_6.7_spmd, body=%wide.region_5.6_spmd.sunk | while | flops 795650 | bytes 3207305 | solution.py:11
  193.9 1.7 fusion.74
  195.7 1.7 fusion.74
  197.5 1.7 fusion.74
  199.3 1.7 fusion.74
  201.1 1.7 fusion.74
  202.9 1.7 fusion.74
  204.7 1.7 fusion.74
  (59 shorter events, 7.0 us)
Async XLA Ops:
  7.2 143.0 %all-gather.5.cloned.1.call-start = ((), (), s32[]{:S(2)}) async-start(), calls=%async_computation.1 | async-start | bytes 4718592 | tf_op jit(solution)/shard_map/all_gather | solution.py:8
  114.2 74.5 %all-gather.3.cloned.1.call-start = ((), (), s32[]{:S(2)}) async-start(), calls=%async_computation | async-start | bytes 4718592 | tf_op jit(solution)/shard_map/all_gather | solution.py:8
  123.8 31.5 %copy-start = (f32[8,1,1024]{2,1,0:T(1,128)}, f32[8,1,1024]{2,1,0:T(1,128)S(1)}, u32[]{:S(2)}) copy-start(f32[8,1,1024]{2,1,0:T(1,128)S(1)} %all_gather.40) | copy-start | bytes 98308
  132.4 22.9 %copy-start.1 = (f32[8,1,1024]{2,1,0:T(1,128)}, f32[8,1,1024]{2,1,0:T(1,128)S(1)}, u32[]{:S(2)}) copy-start(f32[8,1,1024]{2,1,0:T(1,128)S(1)} %all_gather.39) | copy-start | bytes 98308
  141.4 13.9 %copy-start.2 = (f32[8,1,1024]{2,1,0:T(1,128)}, f32[8,1,1024]{2,1,0:T(1,128)S(1)}, u32[]{:S(2)}) copy-start(f32[8,1,1024]{2,1,0:T(1,128)S(1)} %all_gather.43) | copy-start | bytes 98308
  188.7 5.2 %slice-start = ((f32[8,1,1024]{2,1,0:T(1,128)}), f32[7,1,1024]{2,1,0:T(1,128)S(1)}, s32[]{:S(2)}) async-start(f32[8,1,1024]{2,1,0:T(1,128)} %copy-done), calls=%async_computation.2 | async-start | bytes 57344 | tf_op jit(solution)/shard_map/slice | solution.py:10
  188.7 5.2 %slice-start.1 = ((f32[8,1,1024]{2,1,0:T(1,128)}), f32[7,1,1024]{2,1,0:T(1,128)S(1)}, s32[]{:S(2)}) async-start(f32[8,1,1024]{2,1,0:T(1,128)} %copy-done.1), calls=%async_computation.3 | async-start | bytes 57344 | tf_op jit(solution)/shard_map/slice | solution.py:10
  188.7 5.2 %slice-start.2 = ((f32[8,1,1024]{2,1,0:T(1,128)}), f32[7,1,1024]{2,1,0:T(1,128)S(1)}, s32[]{:S(2)}) async-start(f32[8,1,1024]{2,1,0:T(1,128)} %copy-done.2), calls=%async_computation.4 | async-start | bytes 57344 | tf_op jit(solution)/shard_map/slice | solution.py:10
Sparse Core Ops, SparseCore 0:
  114.3 35.8 all-gather.4
  152.1 36.5 all-gather.2
where the time goes:
time: 215 us; the launch traced here: 214 us
  blocking collectives  109 us (51%)
  waiting for transfers between devices  42.8 us (20%)
  matrix products  23.9 us (11%)
  between operations  14.1 us (7%)
  other arithmetic  13.6 us (6%)
  local copies, waits for them, and re-layouts  10.6 us (5%)
    all_gather x2, waiting for transfers between devices, combined_all(): pieces = jax.tree.map(lambda part: lax.all_gather(part, axis), value)  42.1 us
    all_gather x3, blocking collectives, combined_all(): pieces = jax.tree.map(lambda part: lax.all_gather(part, axis), value)  26.4 us
    all_gather x1, blocking collectives, body(): piece_dv = lax.all_gather(tangent_v, 'pb', axis=1, tiled=True)  16.6 us
    all_gather x1, blocking collectives, body(): piece_k = lax.all_gather(keys, 'pb', axis=1, tiled=True)  15.9 us
    all_gather x1, blocking collectives, body(): piece_v = lax.all_gather(values, 'pb', axis=1, tiled=True)  14.9 us
    all_gather x1, blocking collectives, body(): piece_dk = lax.all_gather(tangent_k, 'pb', axis=1, tiled=True)  14 us
    add x7, other arithmetic, join_partials(): tnumer = first[3] * left[..., None] + second[3] * right[..., None]  11.9 us
    all_gather x1, blocking collectives, body(): lax.all_gather(tangent_q, 'ka', axis=1, tiled=True)  10.8 us
  transfers between devices with their start and end apart: 2, of which 2 were waited for; matrix products, arithmetic and copies ran while one was open for 2% of the time, Pallas kernels for 0%

commit v1 on v0

--- a/solution.py
+++ b/solution.py
@@ -2,6 +2,12 @@
 import jax.numpy as jnp
 from jax import lax
 from jax.sharding import PartitionSpec as P
+from jax.lax import all_gather
+
+
+def entries_pass(arr_in):
+    moved = jnp.concatenate(all_gather(arr_in, axis_name="pb"), 1)
+    return moved
 
 
 def combined_all(value, axis, join):
@@ -46,7 +52,7 @@
     piece_k = lax.all_gather(keys, "pb", axis=1, tiled=True)
     piece_dk = lax.all_gather(tangent_k, "pb", axis=1, tiled=True)
     piece_v = lax.all_gather(values, "pb", axis=1, tiled=True)
-    piece_dv = lax.all_gather(tangent_v, "pb", axis=1, tiled=True)
+    piece_dv = entries_pass(tangent_v)
     shaped = (
         start_state[0].reshape(head_count, blocks, block),
         start_state[1].reshape(head_count, blocks, block),

time: 215 us -> 215 us (level)
  no operation moved by 1% of the time
where the time goes in v1:
time: 215 us; the launch traced here: 214 us
  blocking collectives  109 us (51%)
  waiting for transfers between devices  42.8 us (20%)
  matrix products  23.9 us (11%)
  between operations  14.1 us (7%)
  other arithmetic  13.6 us (6%)
  local copies, waits for them, and re-layouts  10.6 us (5%)
    all_gather x2, waiting for transfers between devices, combined_all(): pieces = jax.tree.map(lambda part: lax.all_gather(part, axis), value)  42.1 us
    all_gather x3, blocking collectives, combined_all(): pieces = jax.tree.map(lambda part: lax.all_gather(part, axis), value)  26.4 us
    all_gather x1, blocking collectives, entries_pass(): moved = jnp.concatenate(all_gather(arr_in, axis_name='pb'), 1)  16.6 us
    all_gather x1, blocking collectives, body(): piece_k = lax.all_gather(keys, 'pb', axis=1, tiled=True)  15.9 us
    all_gather x1, blocking collectives, body(): piece_v = lax.all_gather(values, 'pb', axis=1, tiled=True)  14.9 us
    all_gather x1, blocking collectives, body(): piece_dk = lax.all_gather(tangent_k, 'pb', axis=1, tiled=True)  14 us
    add x7, other arithmetic, join_partials(): tnumer = first[3] * left[..., None] + second[3] * right[..., None]  11.9 us
    all_gather x1, blocking collectives, body(): lax.all_gather(tangent_q, 'ka', axis=1, tiled=True)  10.8 us
  transfers between devices with their start and end apart: 2, of which 2 were waited for; matrix products, arithmetic and copies ran while one was open for 2% of the time, Pallas kernels for 0%

profile of v1, /device:TPU:0, one launch (start us, length us, event | category | flops | bytes accessed | tf_op | source)
XLA Modules:
  0.0 214.0 jit_solution(3189630060393108370)
XLA Ops:
  7.3 15.9 %all_gather.37 = f32[1,512,128]{2,1,0:T(8,128)S(1)} all-gather(f32[1,128,128]{2,1,0:T(8,128)} %param.11), channel_id=1, replica_groups=mesh['pb'=4,'ka'=8] {'pb'}, dimensions={1}, use_global_device_ids=true | all-gather | bytes 327680 | tf_op jit(solution)/shard_map/all_gather | solution.py:52
  23.1 14.9 %all_gather.38 = f32[1,512,128]{2,1,0:T(8,128)S(1)} all-gather(f32[1,128,128]{2,1,0:T(8,128)} %param.12), channel_id=1, replica_groups=mesh['pb'=4,'ka'=8] {'pb'}, dimensions={1}, use_global_device_ids=true | all-gather | bytes 327680 | tf_op jit(solution)/shard_map/all_gather | solution.py:54
  38.0 14.0 %all_gather.42 = f32[1,512,128]{2,1,0:T(8,128)S(1)} all-gather(f32[1,128,128]{2,1,0:T(8,128)} %param.14), channel_id=1, replica_groups=mesh['pb'=4,'ka'=8] {'pb'}, dimensions={1}, use_global_device_ids=true | all-gather | bytes 327680 | tf_op jit(solution)/shard_map/all_gather | solution.py:53
  52.1 16.6 %all-gather = f32[4,128,128]{2,1,0:T(8,128)} all-gather(f32[1,128,128]{2,1,0:T(8,128)} %param.15), channel_id=2, replica_groups=mesh['pb'=4,'ka'=8] {'pb'}, dimensions={0}, use_global_device_ids=true | all-gather | bytes 327680 | tf_op jit(solution)/shard_map/all_gather | solution.py:9
  68.6 10.1 %all_gather.36 = f32[1,1024,128]{2,1,0:T(8,128)S(1)} all-gather(f32[1,128,128]{2,1,0:T(8,128)} %param.10), channel_id=1, replica_groups=mesh['pb'=4,'ka'=8] {'ka'}, dimensions={1}, use_global_device_ids=true | all-gather | bytes 589824 | tf_op jit(solution)/shard_map/all_gather | solution.py:37
  78.8 10.8 %all_gather.41 = f32[1,1024,128]{2,1,0:T(8,128)} all-gather(f32[1,128,128]{2,1,0:T(8,128)} %param.13), channel_id=1, replica_groups=mesh['pb'=4,'ka'=8] {'ka'}, dimensions={1}, use_global_device_ids=true | all-gather | bytes 589824 | tf_op jit(solution)/shard_map/all_gather | solution.py:38
  89.5 24.6 %while.53 = (s32[]{:T(128)}, f32[2,512]{1,0:T(2,128)S(1)}, f32[2,512]{1,0:T(2,128)S(1)}, f32[2,512,128]{2,1,0:T(8,128)}, f32[2,512,128]{2,1,0:T(8,128)}, /*index...) while((s32[]{:T(128)}, f32[2,512]{1,0:T(2,128)S(1)}, ...), condition=%wide.region_4.5_spmd, body=%wide.region_0.4_spmd.sunk | while | flops 2419001344 | bytes 12892333 | solution.py:100
  89.5 1.9 fusion.66
  92.7 1.2 fusion.67
  94.0 2.8 %convolution_add_fusion.5 = f32[512,128]{1,0:T(8,128)S(1)} fusion(f32[512,128]{1,0:T(8,128)} %get-tuple-element.549, f32[512,512]{0,1:T(8,128)S(1)} %get-tuple-element.489, f32[512]{0:T(512)S(1)} %get-tuple-element.488, f32[512]{0:T(512)S(1)} %get-tuple-element.492), kind=kOutput, calls=%fused_computation.7.clone.1 | convolution fusion | flops 402980864 | bytes 1576960 | tf_op jit(solution)/shard_map/while/body/eval_jaxpr/while/body/eval_jaxpr/dot_general | solution.py:94
  96.8 2.5 %fusion.71 = f32[2,512,128]{2,1,0:T(8,128)} fusion(f32[2,512,128]{2,1,0:T(8,128)} %get-tuple-element.530, s32[]{:T(128)S(6)} %copy.19, f32[512,128]{1,0:T(8,128)S(1)} %convolution_add_fusion.5, f32[512,512]{0,1:T(8,128)S(1)} %get-tuple-element.493, f32[512,128]{1,0:T(8,128)S(1)} %get-tuple-element.548), kind=kOutput, calls=%fused_computation.6.clone.1 | convolution fusion | flops 402718720 | bytes 1835012 | tf_op jit(solution)/shard_map/while/body/eval_jaxpr/while/body/eval_jaxpr/dot_general | solution.py:95
  99.3 2.5 %fusion.70 = f32[2,512,128]{2,1,0:T(8,128)} fusion(f32[2,512,128]{2,1,0:T(8,128)} %get-tuple-element.529, s32[]{:T(128)S(6)} %copy.19, f32[512,128]{1,0:T(8,128)S(1)} %get-tuple-element.548, f32[512,512]{0,1:T(8,128)S(1)} %get-tuple-element.489, f32[512]{0:T(512)S(1)} %get-tuple-element.488, f32[512]{0:T(512)S(1)} %get-tuple-element.492), kind=kOutput, calls=%fused_computation.10.clone.1 | convolution fusion | flops 402980864 | bytes 1576964 | tf_op jit(solution)/shard_map/while/body/eval_jaxpr/while/body/eval_jaxpr/dot_general | solution.py:91
  101.9 1.9 fusion.66
  105.1 1.2 fusion.67
  106.4 2.8 %convolution_add_fusion.5 = f32[512,128]{1,0:T(8,128)S(1)} fusion(f32[512,128]{1,0:T(8,128)} %get-tuple-element.549, f32[512,512]{0,1:T(8,128)S(1)} %get-tuple-element.489, f32[512]{0:T(512)S(1)} %get-tuple-element.488, f32[512]{0:T(512)S(1)} %get-tuple-element.492), kind=kOutput, calls=%fused_computation.7.clone.1 | convolution fusion | flops 402980864 | bytes 1576960 | tf_op jit(solution)/shard_map/while/body/eval_jaxpr/while/body/eval_jaxpr/dot_general | solution.py:94
  109.1 2.5 %fusion.71 = f32[2,512,128]{2,1,0:T(8,128)} fusion(f32[2,512,128]{2,1,0:T(8,128)} %get-tuple-element.530, s32[]{:T(128)S(6)} %copy.19, f32[512,128]{1,0:T(8,128)S(1)} %convolution_add_fusion.5, f32[512,512]{0,1:T(8,128)S(1)} %get-tuple-element.493, f32[512,128]{1,0:T(8,128)S(1)} %get-tuple-element.548), kind=kOutput, calls=%fused_computation.6.clone.1 | convolution fusion | flops 402718720 | bytes 1835012 | tf_op jit(solution)/shard_map/while/body/eval_jaxpr/while/body/eval_jaxpr/dot_general | solution.py:95
  111.7 2.5 %fusion.70 = f32[2,512,128]{2,1,0:T(8,128)} fusion(f32[2,512,128]{2,1,0:T(8,128)} %get-tuple-element.529, s32[]{:T(128)S(6)} %copy.19, f32[512,128]{1,0:T(8,128)S(1)} %get-tuple-element.548, f32[512,512]{0,1:T(8,128)S(1)} %get-tuple-element.489, f32[512]{0:T(512)S(1)} %get-tuple-element.488, f32[512]{0:T(512)S(1)} %get-tuple-element.492), kind=kOutput, calls=%fused_computation.10.clone.1 | convolution fusion | flops 402980864 | bytes 1576964 | tf_op jit(solution)/shard_map/while/body/eval_jaxpr/while/body/eval_jaxpr/dot_general | solution.py:91
  115.0 8.8 %all_gather.44 = f32[8,1,1024]{2,1,0:T(1,128)S(1)} all-gather(f32[1,1,1024]{2,1,0:T(1,128)S(1)} %all_gather_reshape.16), channel_id=1, replica_groups=mesh['pb'=4,'ka'=8] {'ka'}, dimensions={0}, use_global_device_ids=true | all-gather | bytes 36864 | tf_op jit(solution)/shard_map/all_gather | solution.py:14
  123.8 8.6 %all_gather.43 = f32[8,1,1024]{2,1,0:T(1,128)S(1)} all-gather(f32[1,1,1024]{2,1,0:T(1,128)S(1)} %all_gather_reshape.15), channel_id=1, replica_groups=mesh['pb'=4,'ka'=8] {'ka'}, dimensions={0}, use_global_device_ids=true | all-gather | bytes 36864 | tf_op jit(solution)/shard_map/all_gather | solution.py:14
  132.4 9.0 %all_gather.47 = f32[8,1,1024]{2,1,0:T(1,128)S(1)} all-gather(f32[1,1,1024]{2,1,0:T(1,128)S(1)} %all_gather_reshape.19), channel_id=1, replica_groups=mesh['pb'=4,'ka'=8] {'ka'}, dimensions={0}, use_global_device_ids=true | all-gather | bytes 36864 | tf_op jit(solution)/shard_map/all_gather | solution.py:14
  141.4 8.8 %all-gather.6.cloned.1.call-done = f32[8,1,1024,128]{3,2,1,0:T(8,128)} async-done(((f32[1,1,1024,128]{3,2,1,0:T(8,128)}), f32[8,1,1024,128]{3,2,1,0:T(8,128)}) %all-gather.6.cloned.1.call-update) | async-done | bytes 4194320 | tf_op jit(solution)/shard_map/all_gather | solution.py:14
  150.2 4.1 %slice.48 = f32[7,1,1024,128]{3,2,1,0:T(8,128)} slice(f32[8,1,1024,128]{3,2,1,0:T(8,128)} %all-gather.6.cloned.1.call-done), slice={[1:8], [0:1], [0:1024], [0:128]} | slice | bytes 7340032 | tf_op jit(solution)/shard_map/slice | solution.py:16
  155.4 33.3 %all-gather.4.cloned.1.call-done = f32[8,1,1024,128]{3,2,1,0:T(8,128)} async-done(((f32[1,1,1024,128]{3,2,1,0:T(8,128)}), f32[8,1,1024,128]{3,2,1,0:T(8,128)}) %all-gather.4.cloned.1.call-update) | async-done | bytes 4194320 | tf_op jit(solution)/shard_map/all_gather | solution.py:14
  189.8 4.1 %slice.47 = f32[7,1,1024,128]{3,2,1,0:T(8,128)} slice(f32[8,1,1024,128]{3,2,1,0:T(8,128)} %all-gather.4.cloned.1.call-done), slice={[1:8], [0:1], [0:1024], [0:128]} | slice | bytes 7340032 | tf_op jit(solution)/shard_map/slice | solution.py:16
  193.8 12.5 %while.54 = (s32[]{:T(128)}, f32[1,1024]{1,0:T(1,128)S(1)}, f32[1,1024]{1,0:T(1,128)S(1)}, f32[1,1024,128]{2,1,0:T(8,128)S(1)}, f32[1,1024,128]{2,1,0:T(8,128)S(...) while((s32[]{:T(128)}, f32[1,1024]{1,0:T(1,128)S(1)}, ...), condition=%wide.region_6.7_spmd, body=%wide.region_5.6_spmd.sunk | while | flops 795650 | bytes 3207305 | solution.py:17
  193.9 1.7 fusion.74
  195.7 1.7 fusion.74
  197.5 1.7 fusion.74
  199.3 1.7 fusion.74
  201.1 1.7 fusion.74
  202.9 1.7 fusion.74
  204.7 1.7 fusion.74
  (59 shorter events, 7.0 us)
Async XLA Ops:
  7.2 143.0 %all-gather.6.cloned.1.call-start = ((), (), s32[]{:S(2)}) async-start(), calls=%async_computation.1 | async-start | bytes 4718592 | tf_op jit(solution)/shard_map/all_gather | solution.py:14
  114.2 74.5 %all-gather.4.cloned.1.call-start = ((), (), s32[]{:S(2)}) async-start(), calls=%async_computation | async-start | bytes 4718592 | tf_op jit(solution)/shard_map/all_gather | solution.py:14
  123.8 31.5 %copy-start = (f32[8,1,1024]{2,1,0:T(1,128)}, f32[8,1,1024]{2,1,0:T(1,128)S(1)}, u32[]{:S(2)}) copy-start(f32[8,1,1024]{2,1,0:T(1,128)S(1)} %all_gather.44) | copy-start | bytes 98308
  132.4 22.9 %copy-start.1 = (f32[8,1,1024]{2,1,0:T(1,128)}, f32[8,1,1024]{2,1,0:T(1,128)S(1)}, u32[]{:S(2)}) copy-start(f32[8,1,1024]{2,1,0:T(1,128)S(1)} %all_gather.43) | copy-start | bytes 98308
  141.4 13.9 %copy-start.2 = (f32[8,1,1024]{2,1,0:T(1,128)}, f32[8,1,1024]{2,1,0:T(1,128)S(1)}, u32[]{:S(2)}) copy-start(f32[8,1,1024]{2,1,0:T(1,128)S(1)} %all_gather.47) | copy-start | bytes 98308
  188.7 5.2 %slice-start = ((f32[8,1,1024]{2,1,0:T(1,128)}), f32[7,1,1024]{2,1,0:T(1,128)S(1)}, s32[]{:S(2)}) async-start(f32[8,1,1024]{2,1,0:T(1,128)} %copy-done), calls=%async_computation.2 | async-start | bytes 57344 | tf_op jit(solution)/shard_map/slice | solution.py:16
  188.7 5.2 %slice-start.1 = ((f32[8,1,1024]{2,1,0:T(1,128)}), f32[7,1,1024]{2,1,0:T(1,128)S(1)}, s32[]{:S(2)}) async-start(f32[8,1,1024]{2,1,0:T(1,128)} %copy-done.1), calls=%async_computation.3 | async-start | bytes 57344 | tf_op jit(solution)/shard_map/slice | solution.py:16
  188.7 5.2 %slice-start.2 = ((f32[8,1,1024]{2,1,0:T(1,128)}), f32[7,1,1024]{2,1,0:T(1,128)S(1)}, s32[]{:S(2)}) async-start(f32[8,1,1024]{2,1,0:T(1,128)} %copy-done.2), calls=%async_computation.4 | async-start | bytes 57344 | tf_op jit(solution)/shard_map/slice | solution.py:16
Sparse Core Ops, SparseCore 0:
  114.3 35.8 all-gather.5
  152.1 36.5 all-gather.3
